TPU v7x, 256 devices: a whole 4x4x8 slice. The times are simulated.
256 devices in a mesh: span: 64 (over y, x, z_lo, core), head: 4 (over z_hi).
Axes of the slice: x: 4, y: 4, z: 8 (z_hi: 4, z_lo: 2; z = z_hi * 2 + z_lo), core: 2. Of those that a mesh axis runs over, the one named last changes fastest.
Arguments:
- decoder_states: bfloat16 [131072, 1024], P('span'), may hold values from -21 to 21
- encodings: bfloat16 [4096, 128, 1024], P('span', 'head'), may hold values from -21 to 21
- neighbor_table: int32 [2048, 2, 2], P('span'), may hold values from 0 to 63, as said below
- query_weight: bfloat16 [1024, 1024], P(None, 'head'), may hold values from -0.1875 to 0.1875
- key_weight: bfloat16 [1024, 1024], P(None, 'head'), may hold values from -0.1875 to 0.1875
- value_weight: bfloat16 [1024, 1024], P(None, 'head'), may hold values from -0.1875 to 0.1875
- out_weight: bfloat16 [1024, 1024], P('head'), may hold values from -0.1875 to 0.1875
Outputs:
- attended: bfloat16 [131072, 1024], P('span', 'head')
Inputs may be any that keep to these rules, and one draw needn't show every extreme that they name: neighbor_table[c, k, 0] is the database shard and neighbor_table[c, k, 1] the slot in that shard of neighbor k of span c; in each aligned block of 32 spans (the spans of one device along `span`) every shard is named by exactly one neighbor, and every slot of every shard is named exactly once in the whole table.
All inputs are finite; a program needn't handle non-finite values.
Results may differ from a plain program's by a relative error of at most 0.012.
The roundings to bfloat16 on the way count: a program that leaves them out, or rounds other values in their place, can miss the bound.
Values may be sent and summed in bfloat16 or wider, within the bound.
A program may use at most 128 MiB of HBM per device.

v0:
```python
import jax
import jax.numpy as jnp
from jax import lax
from jax.sharding import PartitionSpec as P

HEAD_DIM = 64
SPAN_LEN = 64
SEQ_LEN = 2048


def body(
    decoder_states, encodings, neighbor_table, query_weight, key_weight, value_weight, out_weight
):
    peer_count = lax.axis_size("span")
    column_rows = lax.all_to_all(out_weight, "head", split_axis=1, concat_axis=0, tiled=True)
    shard_ids = neighbor_table[:, :, 0].reshape(-1)
    slot_ids = neighbor_table[:, :, 1].reshape(-1)
    entries = shard_ids.shape[0]
    per_peer = entries // peer_count
    numbering = jnp.arange(entries, dtype=jnp.int32)
    same_before = (shard_ids[:, None] == shard_ids[None, :]) & (
        numbering[None, :] < numbering[:, None]
    )
    ranking = jnp.sum(same_before.astype(jnp.int32), axis=1)
    position = shard_ids * per_peer + ranking
    placed = position[None, :] == numbering[:, None]
    request = jnp.sum(jnp.where(placed, slot_ids[None, :], 0), axis=1)
    wanted = lax.all_to_all(request, "span", split_axis=0, concat_axis=0, tiled=True)
    selected = encodings[wanted]
    model_width = decoder_states.shape[1]
    group_cols = query_weight.shape[1]
    both_weights = jnp.concatenate([key_weight, value_weight], axis=1)
    arrived = lax.all_to_all(selected, "span", split_axis=0, concat_axis=0, tiled=True)
    block_in = lax.all_gather(arrived, "head", axis=1, tiled=True)
    flattened = block_in.reshape(-1, model_width)
    result = jnp.dot(flattened, both_weights, preferred_element_type=jnp.float32).astype(
        jnp.bfloat16
    )
    projected = result.reshape(block_in.shape[0], block_in.shape[1], 2 * group_cols)
    ordered = projected[position]
    span_count = neighbor_table.shape[0]
    neighbors = neighbor_table.shape[1]
    heads_here = group_cols // HEAD_DIM
    ordered = ordered.reshape(span_count, neighbors * projected.shape[1], 2 * group_cols)
    key_rows = ordered[:, :, :group_cols].reshape(span_count, -1, heads_here, HEAD_DIM)
    value_rows = ordered[:, :, group_cols:].reshape(span_count, -1, heads_here, HEAD_DIM)
    queries = jnp.dot(decoder_states, query_weight, preferred_element_type=jnp.float32).astype(
        jnp.bfloat16
    )
    sequences = decoder_states.shape[0] // SEQ_LEN
    offset = SPAN_LEN - 1
    queries = queries.reshape(sequences, SEQ_LEN, group_cols)
    shifted = jnp.concatenate(
        [queries[:, offset:], jnp.zeros((sequences, offset, group_cols), jnp.bfloat16)], axis=1
    )
    shifted = shifted.reshape(span_count, SPAN_LEN, heads_here, HEAD_DIM)
    inv_root = HEAD_DIM ** (-0.5)
    scores = (
        jnp.einsum("cqhd,ckhd->chqk", shifted, key_rows, preferred_element_type=jnp.float32)
        * inv_root
    )
    weights = jax.nn.softmax(scores, axis=-1).astype(jnp.bfloat16)
    context = jnp.einsum(
        "chqk,ckhd->cqhd", weights, value_rows, preferred_element_type=jnp.float32
    ).astype(jnp.bfloat16)
    context = context.reshape(sequences, SEQ_LEN, group_cols)
    context = jnp.concatenate(
        [jnp.zeros((sequences, offset, group_cols), jnp.bfloat16), context[:, : SEQ_LEN - offset]],
        axis=1,
    )
    context = context.reshape(-1, group_cols)
    summed = jnp.dot(
        lax.all_gather(context, "head", axis=1, tiled=True),
        column_rows,
        preferred_element_type=jnp.float32,
    )
    return summed.astype(jnp.bfloat16)


def solution(mesh):
    return jax.shard_map(
        body,
        mesh=mesh,
        in_specs=(
            P("span", None),
            P("span", "head", None),
            P("span", None, None),
            P(None, "head"),
            P(None, "head"),
            P(None, "head"),
            P("head", None),
        ),
        out_specs=P("span", "head"),
        check_vma=False,
    )
```

profile of v0, /device:TPU:33, one launch (start us, length us, event | category | flops | bytes accessed | tf_op | source)
XLA Modules:
  0.0 560.3 jit_solution(16839109739039627777)
XLA Ops:
  6.5 0.0 copy-start
  6.5 0.0 all-gather.4.cloned.1.call-start
  6.5 0.8 fusion.30
  7.3 0.1 copy.50
  7.4 0.1 reshape_squeeze.5
  7.5 0.2 convert_reduce_fusion
  7.7 0.1 copy.51
  7.8 0.1 broadcast_in_dim.14
  7.9 0.1 select_reduce_fusion
  8.0 0.1 copy.52
  8.1 15.8 %all_to_all.36 = s32[64,1,1]{2,1,0:T(1,128)S(1)} all-to-all(s32[64,1,1]{2,1,0:T(1,128)S(1)} %copy.52), channel_id=1, replica_groups=mesh['span'=64,'head'=4] {'span'}, dimensions={0} | all-to-all | bytes 512 | tf_op jit(solution)/shard_map/all_to_all | solution.py:28
  23.9 1.2 reduce
  25.1 4.9 gather_fusion
  30.1 56.3 %all_to_all.37 = bf16[64,32,1024]{2,1,0:T(8,128)(2,1)} all-to-all(bf16[64,32,1024]{2,1,0:T(8,128)(2,1)} %gather_fusion), channel_id=1, replica_groups=mesh['span'=64,'head'=4] {'span'}, dimensions={0} | all-to-all | bytes 8388608 | tf_op jit(solution)/shard_map/all_to_all | solution.py:33
  86.4 0.0 all-gather.4.cloned.1.call-update
  86.4 0.2 all-gather.6.cloned.1.call-start
  86.6 0.1 reshape_squeeze.6
  86.7 0.0 copy-done
  86.7 3.4 fusion.11
  90.2 0.0 copy-start.4
  90.2 0.2 slice.29
  90.4 1.0 concatenate.10
  91.5 3.3 reshape.100
  94.8 285.4 %all-gather.4.cloned.1.call-done = bf16[64,128,1024]{2,1,0:T(8,128)(2,1)} async-done(((bf16[64,32,1024]{2,1,0:T(8,128)(2,1)}), bf16[64,128,1024]{2,1,0:T(8,128)(2,1)}) %all-gather.4.cloned.1.call-update) | async-done | bytes 16777232 | tf_op jit(solution)/shard_map/all_gather | solution.py:34
  380.3 0.0 copy-done.4
  380.3 14.5 %convolution_convert_fusion = bf16[8192,512]{1,0:T(8,128)(2,1)} fusion(bf16[8192,1024]{1,0:T(8,128)(2,1)} %bitcast.54, bf16[1024,256]{1,0:T(8,128)(2,1)S(1)} %copy-done.4, bf16[1024,256]{1,0:T(8,128)(2,1)} %param.11), kind=kOutput, calls=%fused_computation.3 | convolution fusion | flops 8596226048 | bytes 26214400 | tf_op jit(solution)/shard_map/dot_general | solution.py:36
  394.8 8.9 %gather_fusion.1 = bf16[64,128,512]{2,1,0:T(8,128)(2,1)} fusion(bf16[64,128,512]{2,1,0:T(8,128)(2,1)} %bitcast.47, s32[1024]{0:T(1024)S(1)} %pad_clamp_fusion), kind=kCustom, calls=%fused_computation.1 | custom fusion | bytes 16777472 | tf_op jit(solution)/shard_map/gather | solution.py:40
  403.7 5.9 %fusion.29 = (bf16[32,256,256]{2,1,0:T(8,128)(2,1)}, bf16[32,256,256]{2,1,0:T(8,128)(2,1)}) fusion(bf16[32,256,512]{2,1,0:T(8,128)(2,1)} %bitcast.45), kind=kLoop, calls=%fused_computation.37 | loop fusion | bytes 16777216 | tf_op jit(solution)/shard_map/slice | solution.py:45
  409.6 6.4 %copy.61 = bf16[32,256,256]{1,2,0:T(8,128)(2,1)} copy(bf16[32,256,256]{2,1,0:T(8,128)(2,1)} %get-tuple-element.5) | data formatting | bytes 8388608
  416.0 3.4 fusion.12
  419.4 0.0 copy-start.2
  419.4 3.1 fusion.31
  422.6 0.1 copy-done.2
  422.6 6.4 %copy.60 = bf16[32,256,256]{1,2,0:T(8,128)(2,1)} copy(bf16[32,256,256]{2,1,0:T(8,128)(2,1)} %get-tuple-element.6) | data formatting | bytes 8388608
  429.0 22.4 %convert_bitcast_fusion = bf16[32,64,4,64]{1,3,2,0:T(8,128)(2,1)} fusion(bf16[32,256,4,64]{1,3,2,0:T(8,128)(2,1)} %bitcast.49, f32[32,4,64]{2,1,0:T(4,128)S(1)} %fusion.31, f32[32,4,64,256]{3,2,1,0:T(8,128)} %copy-done.2), kind=kOutput, calls=%fused_computation.17 | convolution fusion | flops 279453952 | bytes 13664256 | tf_op jit(solution)/shard_map/chqk,ckhd->cqhd/dot_general | solution.py:63
  451.4 2.9 copy.57
  454.4 0.0 copy-start.3
  454.4 2.4 reshape.102
  456.8 2.6 concatenate.11
  459.4 0.0 all-gather.6.cloned.1.call-update
  459.5 0.0 copy-done.3
  459.5 0.2 copy.58
  459.7 16.1 %all_to_all.38 = bf16[256,4,256]{0,2,1:T(8,128)(2,1)S(1)} all-to-all(bf16[256,4,256]{0,2,1:T(8,128)(2,1)S(1)} %bitcast.51), channel_id=1, replica_groups=mesh['span'=64,'head'=4] {'head'}, dimensions={1} | all-to-all | bytes 1048576 | tf_op jit(solution)/shard_map/all_to_all | solution.py:15
  475.8 0.2 copy.59
  476.0 72.9 %all-gather.6.cloned.1.call-done = bf16[1,2048,1024]{1,2,0:T(8,128)(2,1)} async-done(((bf16[1,2048,256]{1,2,0:T(8,128)(2,1)}), bf16[1,2048,1024]{1,2,0:T(8,128)(2,1)}) %all-gather.6.cloned.1.call-update) | async-done | bytes 4194320 | tf_op jit(solution)/shard_map/all_gather | solution.py:73
  548.9 0.0 copy-start.1
  548.9 4.5 fusion.8
  553.4 0.0 copy-done.1
  (5 shorter events, 0.0 us)
Async XLA Ops:
  6.5 80.2 %copy-start = (bf16[1024,256]{1,0:T(8,128)(2,1)S(1)}, bf16[1024,256]{1,0:T(8,128)(2,1)}, u32[]{:S(2)}) copy-start(bf16[1024,256]{1,0:T(8,128)(2,1)} %param.10) | copy-start | bytes 1572868
  6.5 373.7 %all-gather.4.cloned.1.call-start = ((), (), s32[]{:S(2)}) async-start(), calls=%async_computation.3 | async-start | bytes 20971520 | tf_op jit(solution)/shard_map/all_gather | solution.py:34
  86.4 462.5 %all-gather.6.cloned.1.call-start = ((), (), s32[]{:S(2)}) async-start(), calls=%async_computation.4 | async-start | bytes 5242880 | tf_op jit(solution)/shard_map/all_gather | solution.py:73
  90.2 290.1 %copy-start.4 = (bf16[1024,256]{1,0:T(8,128)(2,1)S(1)}, bf16[1024,256]{1,0:T(8,128)(2,1)}, u32[]{:S(2)}) copy-start(bf16[1024,256]{1,0:T(8,128)(2,1)} %param.12) | copy-start | bytes 1572868
  419.4 3.2 copy-start.2
  454.4 5.1 copy-start.3
  548.9 4.6 copy-start.1
Sparse Core Ops, SparseCore 0:
  86.5 293.6 all-gather.3
  459.6 89.2 all-gather.5
where the time goes:
time: 561 us; the launch traced here: 560 us
  waiting for transfers between devices  358 us (64%)
  blocking collectives  88.2 us (16%)
  matrix products  48.3 us (9%)
  local copies, waits for them, and re-layouts  47 us (8%)
  between operations  13.5 us (2%)
    all_gather x1, waiting for transfers between devices, body(): block_in = lax.all_gather(arrived, 'head', axis=1, tiled=True)  285 us
    all_gather x1, waiting for transfers between devices, body(): lax.all_gather(context, 'head', axis=1, tiled=True)  72.9 us
    all_to_all x1, blocking collectives, body(): lax.all_to_all(selected, 'span', split_axis=0, concat_axis=0, tiled=True)  56.3 us
    dot_general x1, matrix products, body(): jnp.einsum('chqk,ckhd->cqhd', weights, value_rows, preferred_element_type...  22.4 us
    all_to_all x1, blocking collectives, body(): lax.all_to_all(out_weight, 'head', split_axis=1, concat_axis=0, tiled=True)  16.1 us
    all_to_all x1, blocking collectives, body(): lax.all_to_all(request, 'span', split_axis=0, concat_axis=0, tiled=True)  15.8 us
    dot_general x1, matrix products, body(): jnp.dot(flattened, both_weights, preferred_element_type=jnp.float32)  14.5 us
    unnamed x13, local copies, waits for them, and re-layouts  13.1 us
  transfers between devices with their start and end apart: 2, of which 2 were waited for; matrix products, arithmetic and copies ran while one was open for 2% of the time, Pallas kernels for 0%

commit v1 on v0

--- a/solution.py
+++ b/solution.py
@@ -6,6 +6,9 @@
 HEAD_DIM = 64
 SPAN_LEN = 64
 SEQ_LEN = 2048
+number_points_over_axis = lambda unit: jnp.concatenate(
+    lax.all_to_all(jnp.stack([unit for _ in range(lax.psum(1, "head"))]), "head", 0, 0), axis=1
+)
 
 
 def body(
@@ -31,7 +34,7 @@
     group_cols = query_weight.shape[1]
     both_weights = jnp.concatenate([key_weight, value_weight], axis=1)
     arrived = lax.all_to_all(selected, "span", split_axis=0, concat_axis=0, tiled=True)
-    block_in = lax.all_gather(arrived, "head", axis=1, tiled=True)
+    block_in = number_points_over_axis(arrived)
     flattened = block_in.reshape(-1, model_width)
     result = jnp.dot(flattened, both_weights, preferred_element_type=jnp.float32).astype(
         jnp.bfloat16

time: 561 us -> 651 us (1.16)
  blocking collectives: 88.2 us -> 228 us
  waiting for transfers between devices: 358 us -> 291 us
  local copies, waits for them, and re-layouts: 47 us -> 58.9 us
  starting transfers between devices: 0.22 us -> 7.28 us
    all_gather x1 -> x0, waiting for transfers between devices: 285 us -> none  [body(): block_in = lax.all_gather(arrived, 'head', axis=1, tiled=True)]
    all_to_all x0 -> x1, waiting for transfers between devices: none -> 217 us  [lax.all_to_all(jnp.stack([unit for _ in range(lax.psum(1, 'head'))]), 'he...]
    all_to_all x1, blocking collectives: 16.1 us -> 156 us  [body(): lax.all_to_all(out_weight, 'head', split_axis=1, concat_axis=0, tiled=True)]
    all_to_all x0 -> x1, local copies, waits for them, and re-layouts: none -> 8.26 us  [lax.all_to_all(jnp.stack([unit for _ in range(lax.psum(1, 'head'))]), 'he...]
    all_to_all x0 -> x1, starting transfers between devices: none -> 7.28 us  [lax.all_to_all(jnp.stack([unit for _ in range(lax.psum(1, 'head'))]), 'he...]
    unnamed x13 -> x15, local copies, waits for them, and re-layouts: 13.1 us -> 13.2 us
  transfers between devices with their start and end apart: 2 -> 2, of which waited for: 2 -> 2; matrix products, arithmetic and copies ran while one was open for 2% -> 1% of each run, Pallas kernels for 0% -> 0%
where the time goes in v1:
time: 651 us; the launch traced here: 649 us
  waiting for transfers between devices  291 us (45%)
  blocking collectives  228 us (35%)
  local copies, waits for them, and re-layouts  58.9 us (9%)
  matrix products  45.8 us (7%)
  between operations  13.5 us (2%)
  starting transfers between devices  7.28 us (1%)
    all_to_all x1, waiting for transfers between devices, lax.all_to_all(jnp.stack([unit for _ in range(lax.psum(1, 'head'))]), 'he...  217 us
    all_to_all x1, blocking collectives, body(): lax.all_to_all(out_weight, 'head', split_axis=1, concat_axis=0, tiled=True)  156 us
    all_gather x1, waiting for transfers between devices, body(): lax.all_gather(context, 'head', axis=1, tiled=True)  73.6 us
    all_to_all x1, blocking collectives, body(): lax.all_to_all(selected, 'span', split_axis=0, concat_axis=0, tiled=True)  55.6 us
    dot_general x1, matrix products, body(): jnp.einsum('chqk,ckhd->cqhd', weights, value_rows, preferred_element_type...  22.4 us
    all_to_all x1, blocking collectives, body(): lax.all_to_all(request, 'span', split_axis=0, concat_axis=0, tiled=True)  15.8 us
    unnamed x15, local copies, waits for them, and re-layouts  13.2 us
  transfers between devices with their start and end apart: 2, of which 2 were waited for; matrix products, arithmetic and copies ran while one was open for 1% of the time, Pallas kernels for 0%

profile of v1, /device:TPU:33, one launch (start us, length us, event | category | flops | bytes accessed | tf_op | source)
XLA Modules:
  0.0 648.6 jit_solution(4953353238552204917)
XLA Ops:
  6.5 0.0 copy-start
  6.5 0.8 fusion.30
  7.3 0.1 copy.52
  7.4 0.1 reshape_squeeze.5
  7.5 0.2 convert_reduce_fusion
  7.7 0.1 copy.53
  7.8 0.1 broadcast_in_dim.14
  7.9 0.1 select_reduce_fusion
  8.0 0.1 copy.54
  8.1 15.8 %all_to_all.41 = s32[64,1,1]{2,1,0:T(1,128)S(1)} all-to-all(s32[64,1,1]{2,1,0:T(1,128)S(1)} %copy.54), channel_id=1, replica_groups=mesh['span'=64,'head'=4] {'span'}, dimensions={0} | all-to-all | bytes 512 | tf_op jit(solution)/shard_map/all_to_all | solution.py:31
  23.9 1.2 reduce
  25.1 4.9 gather_fusion
  30.1 55.6 %all_to_all.42 = bf16[64,32,1024]{2,1,0:T(8,128)(2,1)S(1)} all-to-all(bf16[64,32,1024]{2,1,0:T(8,128)(2,1)} %gather_fusion), channel_id=1, replica_groups=mesh['span'=64,'head'=4] {'span'}, dimensions={0} | all-to-all | bytes 8388608 | tf_op jit(solution)/shard_map/all_to_all | solution.py:36
  85.6 5.9 stack.2
  91.6 7.3 %all-to-all-start.2 = ((bf16[4,64,32,1024]{3,2,1,0:T(8,128)(2,1)}), bf16[4,64,32,1024]{3,2,1,0:T(8,128)(2,1)}, u32[]{:S(2)}, u32[]{:S(2)}) async-start(bf16[4,64,32,1024]{3,2,1,0:T(8,128)(2,1)} %stack.2), calls=%async_computation.2 | async-start | bytes 33554432 | tf_op jit(solution)/shard_map/all_to_all | solution.py:10
  98.9 0.0 all-gather.3.cloned.1.call-start
  98.9 0.1 reshape_squeeze.6
  99.0 0.0 copy-done
  99.0 3.4 fusion.11
  102.4 0.2 slice.29
  102.7 0.1 concatenate.10
  102.8 1.8 reshape.102
  104.6 0.0 copy-start.5
  104.6 217.2 %all-to-all-done.2 = bf16[4,64,32,1024]{3,2,1,0:T(8,128)(2,1)} async-done(((bf16[4,64,32,1024]{3,2,1,0:T(8,128)(2,1)}), bf16[4,64,32,1024]{3,2,1,0:T(8,128)(2,1)}, u32[]{:S(2)}, u32[]{:S(2)}) %all-to-all-start.2) | async-done | bytes 16777248 | tf_op jit(solution)/shard_map/all_to_all | solution.py:10
  321.8 8.3 %copy.55 = bf16[4,64,32,1024]{3,2,0,1:T(8,128)(2,1)S(1)} copy(bf16[4,64,32,1024]{3,2,1,0:T(8,128)(2,1)} %all-to-all-done.2) | data formatting | bytes 33554432 | tf_op jit(solution)/shard_map/all_to_all | solution.py:10
  330.1 0.0 copy-done.5
  330.1 12.0 %convolution_convert_fusion = bf16[8192,512]{1,0:T(8,128)(2,1)} fusion(bf16[8192,1024]{1,0:T(8,128)(2,1)S(1)} %bitcast.49, bf16[1024,256]{1,0:T(8,128)(2,1)S(1)} %copy-done.5, bf16[1024,256]{1,0:T(8,128)(2,1)} %param.11), kind=kOutput, calls=%fused_computation.3 | convolution fusion | flops 8596226048 | bytes 26214400 | tf_op jit(solution)/shard_map/dot_general | solution.py:39
  342.1 8.9 %gather_fusion.1 = bf16[64,128,512]{2,1,0:T(8,128)(2,1)} fusion(bf16[64,128,512]{2,1,0:T(8,128)(2,1)} %bitcast.50, s32[1024]{0:T(1024)S(1)} %pad_clamp_fusion), kind=kCustom, calls=%fused_computation.1 | custom fusion | bytes 16777472 | tf_op jit(solution)/shard_map/gather | solution.py:43
  351.1 5.9 fusion.29
  357.0 6.6 %copy.64 = bf16[32,256,256]{1,2,0:T(8,128)(2,1)} copy(bf16[32,256,256]{2,1,0:T(8,128)(2,1)} %get-tuple-element.5) | data formatting | bytes 8388608
  363.5 0.0 copy-done.3
  363.5 3.4 fusion.12
  367.0 0.0 copy-start.2
  367.0 3.1 fusion.31
  370.1 0.1 copy-done.2
  370.2 6.4 copy.63
  376.6 22.4 %convert_bitcast_fusion = bf16[32,64,4,64]{1,3,2,0:T(8,128)(2,1)} fusion(bf16[32,256,4,64]{1,3,2,0:T(8,128)(2,1)} %bitcast.52, f32[32,4,64]{2,1,0:T(4,128)S(1)} %fusion.31, f32[32,4,64,256]{3,2,1,0:T(8,128)} %copy-done.2), kind=kOutput, calls=%fused_computation.17 | convolution fusion | flops 279453952 | bytes 13664256 | tf_op jit(solution)/shard_map/chqk,ckhd->cqhd/dot_general | solution.py:66
  399.0 2.9 copy.60
  401.9 0.0 copy-start.4
  401.9 2.4 reshape.104
  404.3 2.6 concatenate.11
  407.0 0.0 all-gather.3.cloned.1.call-update
  407.0 0.0 copy-done.4
  407.0 0.2 copy.61
  407.2 156.2 %all_to_all.43 = bf16[256,4,256]{0,2,1:T(8,128)(2,1)S(1)} all-to-all(bf16[256,4,256]{0,2,1:T(8,128)(2,1)S(1)} %bitcast.54), channel_id=1, replica_groups=mesh['span'=64,'head'=4] {'head'}, dimensions={1} | all-to-all | bytes 1048576 | tf_op jit(solution)/shard_map/all_to_all | solution.py:18
  563.4 0.2 copy.62
  563.6 73.6 %all-gather.3.cloned.1.call-done = bf16[1,2048,1024]{1,2,0:T(8,128)(2,1)} async-done(((bf16[1,2048,256]{1,2,0:T(8,128)(2,1)}), bf16[1,2048,1024]{1,2,0:T(8,128)(2,1)}) %all-gather.3.cloned.1.call-update) | async-done | bytes 4194320 | tf_op jit(solution)/shard_map/all_gather | solution.py:76
  637.2 4.6 fusion.8
  (8 shorter events, 0.0 us)
Async XLA Ops:
  6.5 92.4 %copy-start = (bf16[1024,256]{1,0:T(8,128)(2,1)S(1)}, bf16[1024,256]{1,0:T(8,128)(2,1)}, u32[]{:S(2)}) copy-start(bf16[1024,256]{1,0:T(8,128)(2,1)} %param.10) | copy-start | bytes 1572868
  91.6 230.2 %all-to-all-start.2 = ((bf16[4,64,32,1024]{3,2,1,0:T(8,128)(2,1)}), bf16[4,64,32,1024]{3,2,1,0:T(8,128)(2,1)}, u32[]{:S(2)}, u32[]{:S(2)}) async-start(bf16[4,64,32,1024]{3,2,1,0:T(8,128)(2,1)} %stack.2), calls=%async_computation.2 | async-start | bytes 33554432 | tf_op jit(solution)/shard_map/all_to_all | solution.py:10
  98.9 538.3 %all-gather.3.cloned.1.call-start = ((), (), s32[]{:S(2)}) async-start(), calls=%async_computation.4 | async-start | bytes 5242880 | tf_op jit(solution)/shard_map/all_gather | solution.py:76
  104.6 225.5 %copy-start.5 = (bf16[1024,256]{1,0:T(8,128)(2,1)S(1)}, bf16[1024,256]{1,0:T(8,128)(2,1)}, u32[]{:S(2)}) copy-start(bf16[1024,256]{1,0:T(8,128)(2,1)} %param.12) | copy-start | bytes 1572868
  357.0 6.6 %copy-start.3 = (bf16[32,64,4,64]{3,2,1,0:T(4,128)(2,1)S(1)}, bf16[32,64,4,64]{3,2,1,0:T(4,128)(2,1)}, u32[]{:S(2)}) copy-start(bf16[32,64,4,64]{3,2,1,0:T(4,128)(2,1)} %reshape.102) | copy-start | bytes 3145732
  367.0 3.2 copy-start.2
  401.9 5.1 copy-start.4
  637.2 4.6 copy-start.1
Sparse Core Ops, SparseCore 0:
  407.1 230.0 all-gather.2
